TPU v7x, 32 devices: a whole 2x2x4 slice. The times are simulated.
32 devices in a mesh: bl: 8 (over z, x), tm: 4 (over y, core).
Axes of the slice: x: 2, y: 2, z: 4, core: 2. Of those that a mesh axis runs over, the one named last changes fastest.
Arguments:
- visibility_real: bfloat16 [3072, 16, 1024], P('bl', 'tm'), may hold values from -6 to 6
- visibility_imag: bfloat16 [3072, 16, 1024], P('bl', 'tm'), may hold values from -6 to 6
- weights: int32 [3072, 16], P('bl', 'tm'), may hold values from 0 to 8
- labels: int32 [3072], P('bl'), may hold values from 0 to 511, as said below
- owner_of: int32 [512], replicated, may hold values from 0 to 7, as said below
Outputs:
- bandpower: float32 [512, 1024], P(('bl', 'tm'))
Inputs may be any that keep to these rules, and one draw needn't show every extreme that they name: Of the rows of one device, at most 72 have labels of groups with one owner, and these carry at most 18 different labels; in every draw some owner gets exactly 72 such rows with exactly 18 labels from every device. `owner_of`: every owner owns exactly 64 groups.
All inputs are finite; a program needn't handle non-finite values.
Results may differ from a plain program's by a relative error of at most 0.0003.
Values may be sent and summed in bfloat16 or wider, within the bound.
No kernel may reach another device: no remote copies, remote signals or barrier semaphores. Data moves between devices by JAX's collectives and lax.ppermute only.
A program may use at most 128 MiB of HBM per device.

v0:
```python
import functools
import math

import jax
import jax.numpy as jnp
import numpy as np
from jax import lax
from jax.experimental import pallas as pl
from jax.experimental.pallas import tpu as pltpu
from jax.sharding import PartitionSpec as P


HARRIS = (0.35875, 0.48829, 0.14128, 0.01168)
LANES = 128
SUBLANES = 8
RADIX = 4
HALF = 32768.0
VMEM_GRANT = 24 << 20
VMEM_WHOLE = 67_043_328
EXP_BIAS = 80
BF16 = jnp.bfloat16
F32 = jnp.float32
I32 = jnp.int32


def up_to(value, multiple):
    return -(-value // multiple) * multiple


class Sizes:
    def __init__(self, rows, times, channels, groups, owners, parts):
        self.rows, self.times, self.channels = rows, times, channels
        self.groups, self.owners, self.parts = groups, owners, parts
        self.per_owner = groups // owners
        capacity = 3 * rows // (2 * owners)
        self.distinct = min(capacity // 4, self.per_owner // 2)
        self.whole = self.distinct // SUBLANES * SUBLANES
        self.rest = self.distinct - self.whole
        self.slots = owners * self.distinct
        self.slot_lanes = up_to(self.slots, LANES)
        self.meta_parts = self.slot_lanes // LANES
        self.tiles = channels // LANES
        self.data_rows = self.distinct * self.tiles
        self.fold = rows * times
        self.short = channels // RADIX
        self.share = self.per_owner // parts

    def meta_rows(self, count, ranked):
        return up_to((2 * count + ranked) * self.meta_parts, SUBLANES)

    def block_rows(self, count, ranked):
        return count * self.data_rows + self.meta_rows(count, ranked)

    def runs(self, distance):
        found = []
        if self.whole:
            found.append((distance * self.whole, 0, self.whole))
        if self.rest:
            found.append((self.owners * self.whole + distance * self.rest, self.whole, self.rest))
        return found


def taper_table(channels):
    angle = 2.0 * math.pi / channels * np.arange(channels, dtype=np.float64)
    window = (
        HARRIS[0]
        - HARRIS[1] * np.cos(angle)
        + HARRIS[2] * np.cos(2.0 * angle)
        - HARRIS[3] * np.cos(3.0 * angle)
    )
    window = window / np.sqrt(np.sum(window * window))
    return window.astype(np.float32)[None, :]


def short_tables(short):
    index = np.arange(short)
    angle = 2.0 * math.pi / short * (index[:, None] * index[None, :] % short)
    cosine, sine = np.cos(angle), np.sin(angle)
    table = np.block([[cosine, -sine], [sine, cosine]]).astype(np.float32)
    high = table.astype(BF16)
    low = (table - high.astype(np.float32)).astype(BF16)
    return high, low


def twiddle_table(channels):
    short = channels // RADIX
    angle = 2.0 * math.pi / channels * (np.arange(RADIX)[:, None] * np.arange(short)[None, :])
    return np.concatenate([np.cos(angle), np.sin(angle)], axis=0).astype(np.float32)


def iota(shape, dimension):
    return lax.broadcasted_iota(I32, shape, dimension)


def dot(a, b):
    return jnp.dot(a, b, preferred_element_type=F32)


def dot_rows(a, b):
    return lax.dot_general(a, b, (((1,), (1,)), ((), ())), preferred_element_type=F32)


def flag(condition):
    return jnp.where(condition, 1.0, 0.0).astype(F32)


def joined(rows):
    return jnp.concatenate([rows[i : i + 1] for i in range(rows.shape[0])], axis=1)


def place_groups(z, me, labels_ref, owner_ref, weight_ref):
    distance = joined(owner_ref[...]) ^ me
    hits = flag(iota((z.owners, z.groups), 0) == distance)
    match = flag(iota((z.groups, z.rows), 0) == joined(labels_ref[...])).astype(BF16)
    counts = dot_rows(jnp.ones((SUBLANES, z.rows), BF16), match)
    present = flag(counts[:1] > 0.5)
    before = flag(iota((z.groups, z.groups), 0) < iota((z.groups, z.groups), 1)).astype(BF16)
    stacked = jnp.concatenate([hits, hits * present], axis=0).astype(BF16)
    prefix = dot(stacked, before)
    rank = jnp.sum(hits * prefix[: z.owners], axis=0, keepdims=True)
    order = jnp.sum(hits * prefix[z.owners :], axis=0, keepdims=True)
    near = distance.astype(F32)
    slot = jnp.where(
        order < z.whole,
        near * z.whole + order,
        near * z.rest + (order + (z.owners * z.whole - z.whole)),
    )
    wide = jnp.broadcast_to(slot, (SUBLANES, z.groups)).astype(BF16)
    row_slot = dot(wide, match)
    narrow = jnp.concatenate(
        [row_slot, weight_ref[...].astype(F32), jnp.zeros((SUBLANES - z.times, z.rows), F32)],
        axis=0,
    ).astype(BF16)
    widen = flag(iota((z.rows, z.fold), 1) // z.times == iota((z.rows, z.fold), 0)).astype(BF16)
    spread = dot(narrow, widen).astype(I32)
    slot_hit = flag(
        (iota((z.slot_lanes, z.groups), 0) == slot.astype(I32)) & (present > 0.5)
    ).astype(BF16)
    ranks = jnp.broadcast_to(rank, (SUBLANES, z.groups)).astype(BF16)
    slot_rank = dot_rows(ranks, slot_hit).astype(I32)
    return spread, slot_rank


def make_folder(z, instant, spread):
    lane = iota((1, z.fold), 1)
    weight = spread[SUBLANES + instant : SUBLANES + instant + 1].astype(F32)
    weight = jnp.where(lane % z.times == instant, weight, 0.0)
    return jnp.where(iota((z.slots, z.fold), 0) == spread[:1], weight, 0.0).astype(BF16)


def code_sums(z, sum_real, sum_imag):
    top = jnp.max(jnp.maximum(jnp.abs(sum_real), jnp.abs(sum_imag)), axis=1, keepdims=True)
    mantissa = jnp.maximum(top, 2.0**-EXP_BIAS) * 2.0**EXP_BIAS
    exponent = jnp.zeros_like(top)
    shrink = jnp.ones_like(top)
    for step in (64, 32, 16, 8, 4, 2, 1):
        large = mantissa >= 2.0**step
        mantissa = jnp.where(large, mantissa * 2.0**-step, mantissa)
        exponent = jnp.where(large, exponent + step, exponent)
        shrink = jnp.where(large, shrink * 2.0**-step, shrink)
    digits = jnp.ceil(mantissa * 128.0)
    inverse = (shrink * 2.0**EXP_BIAS) * (2.0**22 / digits)
    code = exponent * 512.0 + digits
    diagonal = iota((z.slots, z.slot_lanes), 0) == iota((z.slots, z.slot_lanes), 1)
    code_row = jnp.sum(jnp.where(diagonal, code, 0.0), axis=0, keepdims=True).astype(I32)
    top_code = 2.0 * HALF - 1.0
    word_real = jnp.minimum(sum_real * inverse + (HALF + 0.5), top_code).astype(I32)
    word_imag = jnp.minimum(sum_imag * inverse + (HALF + 0.5), top_code).astype(I32)
    return (word_real << 16) | word_imag, code_row


def fold_and_code(z, instants, spread, slot_rank, taper_ref, real, imag, outs):
    count = len(instants)
    folders = [make_folder(z, instant, spread) for instant in instants]
    folder = folders[0] if count == 1 else jnp.concatenate(folders, axis=0)
    taper = taper_ref[...]
    sum_real = dot(folder, real) * taper
    sum_imag = dot(folder, imag) * taper
    rows = [] if slot_rank is None else [slot_rank]
    codes = []
    for at in range(count):
        padded = folders[at]
        if z.slot_lanes > z.slots:
            padded = jnp.concatenate(
                [padded, jnp.zeros((z.slot_lanes - z.slots, z.fold), BF16)], axis=0
            )
        rows.append(dot_rows(jnp.ones((SUBLANES, z.fold), BF16), padded).astype(I32))
        mine = slice(at * z.slots, (at + 1) * z.slots)
        word, code_row = code_sums(z, sum_real[mine], sum_imag[mine])
        codes.append(code_row)
        for distance in range(z.owners):
            for slot, place, size in z.runs(distance):
                start = at * z.data_rows + place * z.tiles
                for tile in range(z.tiles):
                    outs[distance][pl.ds(start + tile, size, stride=z.tiles), :] = word[
                        slot : slot + size, tile * LANES : (tile + 1) * LANES
                    ]
    lines = []
    for row in rows + codes:
        for part in range(z.meta_parts):
            lines.append(row[:1, part * LANES : (part + 1) * LANES])
    meta_rows = z.meta_rows(count, slot_rank is not None)
    if meta_rows > len(lines):
        lines.append(jnp.zeros((meta_rows - len(lines), LANES), I32))
    meta = jnp.concatenate(lines, axis=0)
    lane = iota(meta.shape, 0) % z.meta_parts * LANES + iota(meta.shape, 1)
    for distance in range(z.owners):
        mine = lane < 0
        for slot, _, size in z.runs(distance):
            mine = mine | ((lane >= slot) & (lane < slot + size))
        outs[distance][count * z.data_rows :, :] = jnp.where(mine, meta, 0)


def send(z, instants, count, *refs):
    first = instants[0] == 0
    if first:
        me_ref, *refs = refs
    sources, outs, refs = refs[:count], refs[count : count + z.owners], refs[count + z.owners :]
    if first:
        spread_out, *refs = refs
    targets, sems = refs[:count], refs[count]
    copies = [
        pltpu.make_async_copy(source, target, sems.at[i])
        for i, (source, target) in enumerate(zip(sources, targets))
    ]
    for copy in copies:
        copy.start()
    for copy in copies[:-2]:
        copy.wait()
    *small, taper_ref, real, imag = targets
    if first:
        spread, slot_rank = place_groups(z, me_ref[0], *small)
        spread_out[...] = spread
    else:
        spread, slot_rank = small[0][...], None
    for copy in copies[-2:]:
        copy.wait()
    flat = (z.fold, z.channels)
    fold_and_code(
        z,
        instants,
        spread,
        slot_rank,
        taper_ref,
        real[...].reshape(flat),
        imag[...].reshape(flat),
        outs,
    )


def sum_meta(z, blocks, count):
    meta = blocks[0][count * z.data_rows :, :]
    for block in blocks[1:]:
        meta = meta + block[count * z.data_rows :, :]
    return meta


def meta_line(z, meta, which):
    return joined(meta[which * z.meta_parts : (which + 1) * z.meta_parts])


def means(z, at, blocks, rank, weight, code, words):
    lanes = (1, z.slot_lanes)
    exponent = code >> 9
    power = jnp.ones(lanes, F32)
    for bit in range(7):
        power = jnp.where((exponent >> bit) & 1 == 1, power * 2.0 ** (1 << bit), power)
    scale = (code & 511).astype(F32) * power * 2.0 ** -(EXP_BIAS + 22)
    mine = iota((z.per_owner, z.slot_lanes), 0) == rank
    selector = jnp.where(mine, scale, 0.0)[:, : z.slots].astype(BF16)
    total = jnp.sum(jnp.where(mine, weight.astype(F32), 0.0), axis=1, keepdims=True)
    factor = 1.0 / jnp.maximum(total, 1.0)
    for distance, block in enumerate(blocks):
        for slot, place, size in z.runs(distance):
            start = at * z.data_rows + place * z.tiles
            for tile in range(z.tiles):
                words[slot : slot + size, tile * LANES : (tile + 1) * LANES] = block[
                    pl.ds(start + tile, size, stride=z.tiles), :
                ]
    word = words[...]

    def mean(coded):
        value = coded.astype(F32) - HALF
        high = value.astype(BF16)
        low = (value - high.astype(F32)).astype(BF16)
        return (dot(selector, high) + dot(selector, low)) * factor

    real = mean(lax.shift_right_logical(word, jnp.full(word.shape, 16, I32)))
    imag = mean(word & 65535)
    return real, imag


def residues(z, real, imag, twiddle_ref):
    quarter = [
        (real[:, m * z.short : (m + 1) * z.short], imag[:, m * z.short : (m + 1) * z.short])
        for m in range(RADIX)
    ]
    even_sum = [a + b for a, b in zip(quarter[0], quarter[2])]
    even_gap = [a - b for a, b in zip(quarter[0], quarter[2])]
    odd_sum = [a + b for a, b in zip(quarter[1], quarter[3])]
    odd_gap = [a - b for a, b in zip(quarter[1], quarter[3])]
    mixed = [
        (even_sum[0] + odd_sum[0], even_sum[1] + odd_sum[1]),
        (even_gap[0] + odd_gap[1], even_gap[1] - odd_gap[0]),
        (even_sum[0] - odd_sum[0], even_sum[1] - odd_sum[1]),
        (even_gap[0] - odd_gap[1], even_gap[1] + odd_gap[0]),
    ]
    turned = [jnp.concatenate(mixed[0], axis=1)]
    for r in range(1, RADIX):
        cosine = twiddle_ref[r : r + 1, :]
        sine = twiddle_ref[RADIX + r : RADIX + r + 1, :]
        a, b = mixed[r]
        turned.append(jnp.concatenate([a * cosine + b * sine, b * cosine - a * sine], axis=1))
    rows = []
    for part in range(z.parts):
        for r in range(RADIX):
            rows.append(turned[r][part * z.share : (part + 1) * z.share])
    return jnp.concatenate(rows, axis=0)


def transform(data, high_ref, low_ref):
    high = data.astype(BF16)
    low = (data - high.astype(F32)).astype(BF16)
    table = high_ref[...]
    return dot(high, table) + (dot(low, table) + dot(high, low_ref[...]))


def product(z, a, b):
    wide = a * b
    return wide[:, : z.short] + wide[:, z.short :]


def take(z, kind, count, names, *refs):
    held, (*outs, words) = dict(zip(names, refs[: len(names)])), refs[len(names) :]
    blocks = [held[f"block{d}"] for d in range(z.owners)]
    meta = sum_meta(z, blocks, count)
    first = kind == "first"
    rank = meta_line(z, meta if first else held["ranks"][...], 0)
    spectra = []
    for at in range(count):
        weight = meta_line(z, meta, first + at)
        code = meta_line(z, meta, first + count + at)
        real, imag = means(z, at, blocks, rank, weight, code, words)
        data = residues(z, real, imag, held["twiddle"])
        spectra.append(transform(data, held["high"], held["low"]))
    if first:
        outs[0][...] = spectra[0]
        outs[1][...] = meta
        return
    total = product(z, held["prior"][...], spectra[0])
    for earlier, later in zip(spectra[:-1], spectra[1:]):
        total = total + product(z, earlier, later)
    if "running" in names:
        total = total + held["running"][...]
    if kind == "middle":
        outs[0][...] = spectra[-1]
        outs[1][...] = total
        return
    outs[0][...] = total + product(z, spectra[-1], held["following"][...])


def finish(z, parts, out):
    size = RADIX * z.share
    total = parts[:size]
    for part in range(1, z.parts):
        total = total + parts[part * size : (part + 1) * size]
    width = z.short // RADIX
    rows = []
    for block in range(RADIX):
        rows.append(
            jnp.concatenate(
                [
                    total[r * z.share : (r + 1) * z.share, block * width : (block + 1) * width]
                    for r in range(RADIX)
                ],
                axis=1,
            )
        )
    data = jnp.concatenate(rows, axis=0)
    source = iota((z.short, z.short), 0)
    wanted = source % width * RADIX + source // width
    move = flag(iota((z.short, z.short), 1) == wanted).astype(BF16)
    high = data.astype(BF16)
    rest = data - high.astype(F32)
    middle = rest.astype(BF16)
    low = (rest - middle.astype(F32)).astype(BF16)
    moved = dot(high, move) + (dot(middle, move) + dot(low, move))
    for block in range(RADIX):
        out[:, block * z.short : (block + 1) * z.short] = moved[
            block * z.share : (block + 1) * z.share
        ]


VMEM = pl.BlockSpec(memory_space=pltpu.VMEM)
SMEM = pl.BlockSpec(memory_space=pltpu.SMEM)
HBM = pl.BlockSpec(memory_space=pltpu.HBM)


def call(body, specs, shapes, scratch, flops, grant=VMEM_GRANT):
    return pl.pallas_call(
        body,
        in_specs=specs,
        out_specs=jax.tree.map(lambda _: VMEM, shapes),
        out_shape=shapes,
        scratch_shapes=scratch,
        compiler_params=pltpu.CompilerParams(vmem_limit_bytes=grant),
        cost_estimate=pl.CostEstimate(flops=flops, bytes_accessed=1 << 20, transcendentals=0),
    )


def swap(block, axis, distance):
    devices = range(lax.axis_size(axis))
    return lax.ppermute(block, axis, [(i, i ^ distance) for i in devices])


def far_first(count):
    return [*range(count // 2, count), *range(1, count // 2)]


def per_device(visibility_real, visibility_imag, weights, labels, owner_of):
    row_count, times, channels = visibility_real.shape
    z = Sizes(
        row_count,
        times,
        channels,
        owner_of.shape[0],
        lax.axis_size("bl"),
        lax.axis_size("tm"),
    )
    me = lax.axis_index("bl").astype(I32).reshape(1)
    taper = jnp.asarray(taper_table(channels))
    high, low = (jnp.asarray(table) for table in short_tables(z.short))
    twiddle = jnp.asarray(twiddle_table(channels))
    fold_flops = 4 * z.slots * z.fold * channels
    chunks = [(0,), tuple(range(1, times - 1)), (times - 1,)]
    chunks = [chunk for chunk in chunks if chunk]

    def sends(chunk):
        rows = z.block_rows(len(chunk), chunk[0] == 0)
        return [jax.ShapeDtypeStruct((rows, LANES), I32)] * z.owners

    def exchange(blocks):
        moved = {}
        for d in far_first(z.owners):
            moved[d] = swap(blocks[d], "bl", d)
        return [blocks[0]] + [moved[d] for d in range(1, z.owners)]

    def fold(at, inputs, extra_outs):
        chunk = chunks[at]
        return call(
            functools.partial(send, z, chunk, len(inputs)),
            [SMEM] * (at == 0) + [HBM] * len(inputs),
            sends(chunk) + extra_outs,
            [pltpu.VMEM(value.shape, value.dtype) for value in inputs]
            + [pltpu.SemaphoreType.DMA((len(inputs),))],
            fold_flops * len(chunk),
            grant=VMEM_WHOLE,
        )(*([me] * (at == 0)), *inputs)

    large = (taper, visibility_real, visibility_imag)
    places = (
        labels.reshape(row_count // LANES, LANES),
        owner_of.reshape(z.groups // LANES, LANES),
        weights.T,
    )
    spread_shape = jax.ShapeDtypeStruct((2 * SUBLANES, z.fold), I32)
    *blocks, spread = fold(0, places + large, [spread_shape])
    arrived = [exchange(blocks)]
    for at in range(1, len(chunks)):
        arrived.append(exchange(fold(at, (spread,) + large, [])))

    spec_shape = jax.ShapeDtypeStruct((RADIX * z.per_owner, 2 * z.short), F32)
    power_shape = jax.ShapeDtypeStruct((RADIX * z.per_owner, z.short), F32)
    take_flops = 3 * 2 * RADIX * z.per_owner * (2 * z.short) ** 2
    state = {"twiddle": twiddle, "high": high, "low": low}

    def taken(kind, at, shapes, extra):
        inputs = {f"block{d}": block for d, block in enumerate(arrived[at])} | extra
        names = tuple(inputs)
        values = list(inputs.values())
        scratch = [pltpu.VMEM((z.slots, channels), I32)]
        specs = [VMEM] * len(values)
        count = len(chunks[at])
        body = functools.partial(take, z, kind, count, names)
        return call(body, specs, shapes, scratch, take_flops * count)(*values)

    meta_shape = jax.ShapeDtypeStruct((z.meta_rows(1, True), LANES), I32)
    spec, ranks = taken("first", 0, [spec_shape, meta_shape], state)
    following = lax.ppermute(spec, "tm", [(i, i - 1) for i in range(1, z.parts)])
    running = {}
    if len(chunks) > 2:
        spec, power = taken(
            "middle", 1, [spec_shape, power_shape], state | {"ranks": ranks, "prior": spec}
        )
        running = {"running": power}
    (power,) = taken(
        "last",
        len(chunks) - 1,
        [power_shape],
        {"ranks": ranks} | state | {"prior": spec, "following": following} | running,
    )
    gathered = lax.all_to_all(power, "tm", split_axis=0, concat_axis=0, tiled=True)
    return call(
        functools.partial(finish, z),
        [VMEM],
        jax.ShapeDtypeStruct((z.share, channels), F32),
        [],
        1 << 20,
    )(gathered)


def solution(mesh):
    placed = (P("bl", "tm", None), P("bl", "tm", None), P("bl", "tm"), P("bl"), P())
    return jax.shard_map(
        per_device, mesh=mesh, in_specs=placed, out_specs=P(("bl", "tm"), None), check_vma=False
    )
```

profile of v0, /device:TPU:10, one launch (start us, length us, event | category | flops | bytes accessed | tf_op | source)
XLA Modules:
  0.0 120.4 jit_solution(3675082427609193932)
XLA Ops:
  0.0 5.5 %shard_map.91 = (s32[152,128]{1,0:T(8,128)}, s32[152,128]{1,0:T(8,128)}, s32[152,128]{1,0:T(8,128)}, s32[152,128]{1,0:T(8,128)}, s32[152,128]{1,0:T(8,128)}, /*i...) custom-call(s32[1]{0:T(128)} %bitcast.refs_0_, s32[3,128]{1,0:T(4,128)} %bitcast.9, ...), custom_call_target="tpu_custom_call" | custom-call | flops 905969664 | bytes 1048576 | tf_op jit(solution)/shard_map/pallas_call | solution.py:450
  5.5 2.6 %collective-permute-start.10 = (s32[152,128]{1,0:T(8,128)}, s32[152,128]{1,0:T(8,128)S(1)}, u32[]{:S(2)}, u32[]{:S(2)}) collective-permute-start(s32[152,128]{1,0:T(8,128)} %get-tuple-element.47), channel_id=1, source_target_pairs={{0,16},{4,20},{8,24},{12,28},{16,0},{20,4},{24,8},{28,12},{1,17},{... | collective-permute-start | bytes 233480 | tf_op jit(solution)/shard_map/ppermute | solution.py:413
  8.4 1.6 %collective-permute-start.12 = (s32[152,128]{1,0:T(8,128)}, s32[152,128]{1,0:T(8,128)}, u32[]{:S(2)}, u32[]{:S(2)}) collective-permute-start(s32[152,128]{1,0:T(8,128)} %get-tuple-element.49), channel_id=1, source_target_pairs={{0,24},{4,28},{8,16},{12,20},{16,8},{20,12},{24,0},{28,4},{1,25},{... | collective-permute-start | bytes 233480 | tf_op jit(solution)/shard_map/ppermute | solution.py:413
  10.0 1.4 %collective-permute-start.13 = (s32[152,128]{1,0:T(8,128)}, s32[152,128]{1,0:T(8,128)}, u32[]{:S(2)}, u32[]{:S(2)}) collective-permute-start(s32[152,128]{1,0:T(8,128)} %get-tuple-element.50), channel_id=1, source_target_pairs={{0,28},{4,24},{8,20},{12,16},{16,12},{20,8},{24,4},{28,0},{1,29},{... | collective-permute-start | bytes 233480 | tf_op jit(solution)/shard_map/ppermute | solution.py:413
  11.9 4.8 %collective-permute-done.10.refs_4_ = s32[152,128]{1,0:T(8,128)S(1)} collective-permute-done((s32[152,128]{1,0:T(8,128)}, s32[152,128]{1,0:T(8,128)S(1)}, u32[]{:S(2)}, u32[]{:S(2)}) %collective-permute-start.10) | collective-permute-done | bytes 77856 | tf_op jit(solution)/shard_map/ppermute | solution.py:413
  16.7 0.6 copy-done.7
  17.5 0.8 collective-permute-done.11.refs_5_
  18.4 0.6 copy-done.9
  19.0 2.8 %collective-permute-start.9 = (s32[152,128]{1,0:T(8,128)}, s32[152,128]{1,0:T(8,128)}, u32[]{:S(2)}, u32[]{:S(2)}) collective-permute-start(s32[152,128]{1,0:T(8,128)} %get-tuple-element.46), channel_id=1, source_target_pairs={{0,12},{4,8},{8,4},{12,0},{16,28},{20,24},{24,20},{28,16},{1,13},{... | collective-permute-start | bytes 233480 | tf_op jit(solution)/shard_map/ppermute | solution.py:413
  21.8 5.5 %shard_map.92 = (s32[152,128]{1,0:T(8,128)}, s32[152,128]{1,0:T(8,128)}, s32[152,128]{1,0:T(8,128)}, s32[152,128]{1,0:T(8,128)}, s32[152,128]{1,0:T(8,128)}, /*i...) custom-call(s32[16,1536]{1,0:T(8,128)} %get-tuple-element.34.refs_0_, ...), custom_call_target="tpu_custom_call" | custom-call | flops 905969664 | bytes 1048576 | tf_op jit(solution)/shard_map/pallas_call | solution.py:450
  27.3 0.9 collective-permute-start
  28.2 1.0 copy-done
  29.3 1.0 copy-done.3
  30.3 0.9 copy-done.6
  31.2 0.9 copy-done.8
  32.1 0.9 copy-done.10
  33.0 0.7 copy-done.11
  33.7 2.9 %shard_map.93 = (f32[256,512]{1,0:T(8,128)}, s32[8,128]{1,0:T(8,128)S(1)}) custom-call(s32[152,128]{1,0:T(8,128)S(1)} %copy-done.6, s32[152,128]{1,0:T(8,128)} %collective-permute-done.7.refs_1_, s32[152,128]{1,0:T(8,128)} %collective-permute-done.8.refs_2_, s32[152,128]{1,0:T(8,128)} %collective-permute-done.9.refs_3_, s32[152,128]{1,0:T(8,128)S(1)} %copy-done.8, ...), custom_call_target="tpu_custom_call" | custom-call | flops 402653184 | bytes 1048576 | tf_op jit(solution)/shard_map/pallas_call | solution.py:485
  36.5 0.6 copy-done.14
  37.1 1.3 %collective-permute-start.21 = (f32[256,512]{1,0:T(8,128)}, f32[256,512]{1,0:T(8,128)}, u32[]{:S(2)}, u32[]{:S(2)}) collective-permute-start(f32[256,512]{1,0:T(8,128)} %get-tuple-element.60.refs_12_), channel_id=1, source_target_pairs={{1,0},{2,1},{3,2},{5,4},{6,5},{7,6},{9,8},{10,9},{11,10},{13,12},{... | collective-permute-start | bytes 1572872 | tf_op jit(solution)/shard_map/ppermute | solution.py:489
  38.4 6.9 %shard_map.94 = (s32[296,128]{1,0:T(8,128)}, s32[296,128]{1,0:T(8,128)}, s32[296,128]{1,0:T(8,128)}, s32[296,128]{1,0:T(8,128)}, s32[296,128]{1,0:T(8,128)}, /*i...) custom-call(s32[16,1536]{1,0:T(8,128)} %get-tuple-element.34.refs_0_, ...), custom_call_target="tpu_custom_call" | custom-call | flops 1811939328 | bytes 1048576 | tf_op jit(solution)/shard_map/pallas_call | solution.py:450
  45.4 1.3 %collective-permute-start.14 = (s32[296,128]{1,0:T(8,128)}, s32[296,128]{1,0:T(8,128)S(1)}, u32[]{:S(2)}, u32[]{:S(2)}) collective-permute-start(s32[296,128]{1,0:T(8,128)} %get-tuple-element.53), channel_id=1, source_target_pairs={{0,4},{4,0},{8,12},{12,8},{16,20},{20,16},{24,28},{28,24},{1,5},{5... | collective-permute-start | bytes 454664 | tf_op jit(solution)/shard_map/ppermute | solution.py:413
  46.6 2.0 %collective-permute-start.15 = (s32[296,128]{1,0:T(8,128)}, s32[296,128]{1,0:T(8,128)S(1)}, u32[]{:S(2)}, u32[]{:S(2)}) collective-permute-start(s32[296,128]{1,0:T(8,128)} %get-tuple-element.54), channel_id=1, source_target_pairs={{0,8},{4,12},{8,0},{12,4},{16,24},{20,28},{24,16},{28,20},{1,9},{5... | collective-permute-start | bytes 454664 | tf_op jit(solution)/shard_map/ppermute | solution.py:413
  48.9 2.6 %collective-permute-start.2 = (s32[152,128]{1,0:T(8,128)}, s32[152,128]{1,0:T(8,128)S(1)}, u32[]{:S(2)}, u32[]{:S(2)}) collective-permute-start(s32[152,128]{1,0:T(8,128)} %get-tuple-element.38), channel_id=1, source_target_pairs={{0,12},{4,8},{8,4},{12,0},{16,28},{20,24},{24,20},{28,16},{1,13},{... | collective-permute-start | bytes 233480 | tf_op jit(solution)/shard_map/ppermute | solution.py:413
  51.6 7.1 %collective-permute-done.2.refs_3_ = s32[152,128]{1,0:T(8,128)S(1)} collective-permute-done((s32[152,128]{1,0:T(8,128)}, s32[152,128]{1,0:T(8,128)S(1)}, u32[]{:S(2)}, u32[]{:S(2)}) %collective-permute-start.2) | collective-permute-done | bytes 77856 | tf_op jit(solution)/shard_map/ppermute | solution.py:413
  58.7 3.2 %collective-permute-start.17 = (s32[296,128]{1,0:T(8,128)}, s32[296,128]{1,0:T(8,128)S(1)}, u32[]{:S(2)}, u32[]{:S(2)}) collective-permute-start(s32[296,128]{1,0:T(8,128)} %get-tuple-element.56), channel_id=1, source_target_pairs={{0,16},{4,20},{8,24},{12,28},{16,0},{20,4},{24,8},{28,12},{1,17},{... | collective-permute-start | bytes 454664 | tf_op jit(solution)/shard_map/ppermute | solution.py:413
  61.9 0.9 collective-permute-start.18
  62.8 1.7 %collective-permute-start.19 = (s32[296,128]{1,0:T(8,128)}, s32[296,128]{1,0:T(8,128)S(1)}, u32[]{:S(2)}, u32[]{:S(2)}) collective-permute-start(s32[296,128]{1,0:T(8,128)} %get-tuple-element.58), channel_id=1, source_target_pairs={{0,24},{4,28},{8,16},{12,20},{16,8},{20,12},{24,0},{28,4},{1,25},{... | collective-permute-start | bytes 454664 | tf_op jit(solution)/shard_map/ppermute | solution.py:413
  64.5 0.8 collective-permute-start.20
  65.3 13.7 %collective-permute-done.17.refs_4_ = s32[296,128]{1,0:T(8,128)S(1)} collective-permute-done((s32[296,128]{1,0:T(8,128)}, s32[296,128]{1,0:T(8,128)S(1)}, u32[]{:S(2)}, u32[]{:S(2)}) %collective-permute-start.17) | collective-permute-done | bytes 151584 | tf_op jit(solution)/shard_map/ppermute | solution.py:413
  79.0 3.3 %collective-permute-start.3 = (s32[152,128]{1,0:T(8,128)}, s32[152,128]{1,0:T(8,128)S(1)}, u32[]{:S(2)}, u32[]{:S(2)}) collective-permute-start(s32[152,128]{1,0:T(8,128)} %get-tuple-element.39), channel_id=1, source_target_pairs={{0,16},{4,20},{8,24},{12,28},{16,0},{20,4},{24,8},{28,12},{1,17},{... | collective-permute-start | bytes 233480 | tf_op jit(solution)/shard_map/ppermute | solution.py:413
  82.3 1.6 %collective-permute-done.18.refs_5_ = s32[296,128]{1,0:T(8,128)S(1)} collective-permute-done((s32[296,128]{1,0:T(8,128)}, s32[296,128]{1,0:T(8,128)S(1)}, u32[]{:S(2)}, u32[]{:S(2)}) %collective-permute-start.18) | collective-permute-done | bytes 151584 | tf_op jit(solution)/shard_map/ppermute | solution.py:413
  84.0 4.2 %collective-permute-start.4 = (s32[152,128]{1,0:T(8,128)}, s32[152,128]{1,0:T(8,128)S(1)}, u32[]{:S(2)}, u32[]{:S(2)}) collective-permute-start(s32[152,128]{1,0:T(8,128)} %get-tuple-element.40), channel_id=1, source_target_pairs={{0,20},{4,16},{8,28},{12,24},{16,4},{20,0},{24,12},{28,8},{1,21},{... | collective-permute-start | bytes 233480 | tf_op jit(solution)/shard_map/ppermute | solution.py:413
  88.1 0.8 collective-permute-done.19.refs_6_
  89.0 5.6 %collective-permute-start.5 = (s32[152,128]{1,0:T(8,128)}, s32[152,128]{1,0:T(8,128)S(1)}, u32[]{:S(2)}, u32[]{:S(2)}) collective-permute-start(s32[152,128]{1,0:T(8,128)} %get-tuple-element.41), channel_id=1, source_target_pairs={{0,24},{4,28},{8,16},{12,20},{16,8},{20,12},{24,0},{28,4},{1,25},{... | collective-permute-start | bytes 233480 | tf_op jit(solution)/shard_map/ppermute | solution.py:413
  94.6 2.0 %collective-permute-done.20.refs_7_ = s32[296,128]{1,0:T(8,128)S(1)} collective-permute-done((s32[296,128]{1,0:T(8,128)}, s32[296,128]{1,0:T(8,128)S(1)}, u32[]{:S(2)}, u32[]{:S(2)}) %collective-permute-start.20) | collective-permute-done | bytes 151584 | tf_op jit(solution)/shard_map/ppermute | solution.py:413
  96.6 2.2 %collective-permute-start.6 = (s32[152,128]{1,0:T(8,128)}, s32[152,128]{1,0:T(8,128)S(1)}, u32[]{:S(2)}, u32[]{:S(2)}) collective-permute-start(s32[152,128]{1,0:T(8,128)} %get-tuple-element.42), channel_id=1, source_target_pairs={{0,28},{4,24},{8,20},{12,16},{16,12},{20,8},{24,4},{28,0},{1,29},{... | collective-permute-start | bytes 233480 | tf_op jit(solution)/shard_map/ppermute | solution.py:413
  98.7 1.0 copy-done.1
  99.8 1.0 copy-done.4
  100.8 0.7 copy-done.12
  101.5 0.7 copy-done.15
  102.2 0.9 copy-done.16
  103.1 3.1 %shard_map.95 = (f32[256,512]{1,0:T(8,128)S(1)}, f32[256,256]{1,0:T(8,128)S(1)}) custom-call(s32[296,128]{1,0:T(8,128)S(1)} %copy-done.16, s32[296,128]{1,0:T(8,128)S(1)} %collective-permute-done.14.refs_1_, s32[296,128]{1,0:T(8,128)S(1)} %collective-permute-done.15.refs_2_, s32[296,128]{1,0:T(8,128)S(1)} %collective-permute-done.16.refs_3_, ...), custom_call_target="tpu_custom_call" | custom-call | flops 805306368 | bytes 1048576 | tf_op jit(solution)/shard_map/pallas_call | solution.py:485
  106.3 0.9 copy-done.5
  107.2 0.7 copy-done.13
  107.9 2.2 %shard_map.96 = f32[256,256]{1,0:T(8,128)S(1)} custom-call(s32[152,128]{1,0:T(8,128)S(1)} %copy-done.5, s32[152,128]{1,0:T(8,128)} %collective-permute-done.refs_1_, s32[152,128]{1,0:T(8,128)} %collective-permute-done.1.refs_2_, s32[152,128]{1,0:T(8,128)S(1)} %collective-permute-done.2.refs_3_, s32[152,128]{1,0:T(8,128)S(1)} %collective-permute-done.3.refs_4_, ...), custom_call_target="tpu_custom_call" | custom-call | flops 402653184 | bytes 1048576 | tf_op jit(solution)/shard_map/pallas_call | solution.py:485
  110.1 9.4 %all_to_all.11 = f32[4,64,256]{2,1,0:T(8,128)S(1)} all-to-all(f32[4,64,256]{2,1,0:T(8,128)S(1)} %bitcast.6), channel_id=1, replica_groups=mesh['bl'=8,'tm'=4] {'tm'}, dimensions={0} | all-to-all | bytes 524288 | tf_op jit(solution)/shard_map/all_to_all | solution.py:502
  119.5 0.9 shard_map.97
  (38 shorter events, 1.4 us)
Async XLA Ops:
  5.5 11.2 %collective-permute-start.10 = (s32[152,128]{1,0:T(8,128)}, s32[152,128]{1,0:T(8,128)S(1)}, u32[]{:S(2)}, u32[]{:S(2)}) collective-permute-start(s32[152,128]{1,0:T(8,128)} %get-tuple-element.47), channel_id=1, source_target_pairs={{0,16},{4,20},{8,24},{12,28},{16,0},{20,4},{24,8},{28,12},{1,17},{... | collective-permute-start | bytes 233480 | tf_op jit(solution)/shard_map/ppermute | solution.py:413
  8.1 10.2 %collective-permute-start.11 = (s32[152,128]{1,0:T(8,128)}, s32[152,128]{1,0:T(8,128)S(1)}, u32[]{:S(2)}, u32[]{:S(2)}) collective-permute-start(s32[152,128]{1,0:T(8,128)} %get-tuple-element.48), channel_id=1, source_target_pairs={{0,20},{4,16},{8,28},{12,24},{16,4},{20,0},{24,12},{28,8},{1,21},{... | collective-permute-start | bytes 233480 | tf_op jit(solution)/shard_map/ppermute | solution.py:413
  8.4 18.8 %collective-permute-start.12 = (s32[152,128]{1,0:T(8,128)}, s32[152,128]{1,0:T(8,128)}, u32[]{:S(2)}, u32[]{:S(2)}) collective-permute-start(s32[152,128]{1,0:T(8,128)} %get-tuple-element.49), channel_id=1, source_target_pairs={{0,24},{4,28},{8,16},{12,20},{16,8},{20,12},{24,0},{28,4},{1,25},{... | collective-permute-start | bytes 233480 | tf_op jit(solution)/shard_map/ppermute | solution.py:413
  10.0 18.2 %collective-permute-start.13 = (s32[152,128]{1,0:T(8,128)}, s32[152,128]{1,0:T(8,128)}, u32[]{:S(2)}, u32[]{:S(2)}) collective-permute-start(s32[152,128]{1,0:T(8,128)} %get-tuple-element.50), channel_id=1, source_target_pairs={{0,28},{4,24},{8,20},{12,16},{16,12},{20,8},{24,4},{28,0},{1,29},{... | collective-permute-start | bytes 233480 | tf_op jit(solution)/shard_map/ppermute | solution.py:413
  11.4 16.8 %collective-permute-start.7 = (s32[152,128]{1,0:T(8,128)}, s32[152,128]{1,0:T(8,128)}, u32[]{:S(2)}, u32[]{:S(2)}) collective-permute-start(s32[152,128]{1,0:T(8,128)} %get-tuple-element.44), channel_id=1, source_target_pairs={{0,4},{4,0},{8,12},{12,8},{16,20},{20,16},{24,28},{28,24},{1,5},{5... | collective-permute-start | bytes 233480 | tf_op jit(solution)/shard_map/ppermute | solution.py:413
  16.7 0.6 copy-start.7
  17.3 10.9 %collective-permute-start.8 = (s32[152,128]{1,0:T(8,128)}, s32[152,128]{1,0:T(8,128)}, u32[]{:S(2)}, u32[]{:S(2)}) collective-permute-start(s32[152,128]{1,0:T(8,128)} %get-tuple-element.45), channel_id=1, source_target_pairs={{0,8},{4,12},{8,0},{12,4},{16,24},{20,28},{24,16},{28,20},{1,9},{5... | collective-permute-start | bytes 233480 | tf_op jit(solution)/shard_map/ppermute | solution.py:413
  18.4 0.6 copy-start.9
  19.0 9.2 %collective-permute-start.9 = (s32[152,128]{1,0:T(8,128)}, s32[152,128]{1,0:T(8,128)}, u32[]{:S(2)}, u32[]{:S(2)}) collective-permute-start(s32[152,128]{1,0:T(8,128)} %get-tuple-element.46), channel_id=1, source_target_pairs={{0,12},{4,8},{8,4},{12,0},{16,28},{20,24},{24,20},{28,16},{1,13},{... | collective-permute-start | bytes 233480 | tf_op jit(solution)/shard_map/ppermute | solution.py:413
  27.3 21.4 %collective-permute-start = (s32[152,128]{1,0:T(8,128)}, s32[152,128]{1,0:T(8,128)}, u32[]{:S(2)}, u32[]{:S(2)}) collective-permute-start(s32[152,128]{1,0:T(8,128)} %get-tuple-element.36), channel_id=1, source_target_pairs={{0,4},{4,0},{8,12},{12,8},{16,20},{20,16},{24,28},{28,24},{1,5},{5... | collective-permute-start | bytes 233480 | tf_op jit(solution)/shard_map/ppermute | solution.py:413
  28.2 20.8 %collective-permute-start.1 = (s32[152,128]{1,0:T(8,128)}, s32[152,128]{1,0:T(8,128)}, u32[]{:S(2)}, u32[]{:S(2)}) collective-permute-start(s32[152,128]{1,0:T(8,128)} %get-tuple-element.37), channel_id=1, source_target_pairs={{0,8},{4,12},{8,0},{12,4},{16,24},{20,28},{24,16},{28,20},{1,9},{5... | collective-permute-start | bytes 233480 | tf_op jit(solution)/shard_map/ppermute | solution.py:413
  28.2 1.0 copy-start
  29.3 1.0 copy-start.3
  30.3 0.9 copy-start.6
  31.2 0.9 copy-start.8
  32.1 0.9 copy-start.10
  33.0 0.7 copy-start.11
  36.5 0.6 copy-start.14
  37.1 69.1 %collective-permute-start.21 = (f32[256,512]{1,0:T(8,128)}, f32[256,512]{1,0:T(8,128)}, u32[]{:S(2)}, u32[]{:S(2)}) collective-permute-start(f32[256,512]{1,0:T(8,128)} %get-tuple-element.60.refs_12_), channel_id=1, source_target_pairs={{1,0},{2,1},{3,2},{5,4},{6,5},{7,6},{9,8},{10,9},{11,10},{13,12},{... | collective-permute-start | bytes 1572872 | tf_op jit(solution)/shard_map/ppermute | solution.py:489
  45.4 16.5 %collective-permute-start.14 = (s32[296,128]{1,0:T(8,128)}, s32[296,128]{1,0:T(8,128)S(1)}, u32[]{:S(2)}, u32[]{:S(2)}) collective-permute-start(s32[296,128]{1,0:T(8,128)} %get-tuple-element.53), channel_id=1, source_target_pairs={{0,4},{4,0},{8,12},{12,8},{16,20},{20,16},{24,28},{28,24},{1,5},{5... | collective-permute-start | bytes 454664 | tf_op jit(solution)/shard_map/ppermute | solution.py:413
  46.6 16.1 %collective-permute-start.15 = (s32[296,128]{1,0:T(8,128)}, s32[296,128]{1,0:T(8,128)S(1)}, u32[]{:S(2)}, u32[]{:S(2)}) collective-permute-start(s32[296,128]{1,0:T(8,128)} %get-tuple-element.54), channel_id=1, source_target_pairs={{0,8},{4,12},{8,0},{12,4},{16,24},{20,28},{24,16},{28,20},{1,9},{5... | collective-permute-start | bytes 454664 | tf_op jit(solution)/shard_map/ppermute | solution.py:413
  48.6 15.8 %collective-permute-start.16 = (s32[296,128]{1,0:T(8,128)}, s32[296,128]{1,0:T(8,128)S(1)}, u32[]{:S(2)}, u32[]{:S(2)}) collective-permute-start(s32[296,128]{1,0:T(8,128)} %get-tuple-element.55), channel_id=1, source_target_pairs={{0,12},{4,8},{8,4},{12,0},{16,28},{20,24},{24,20},{28,16},{1,13},{... | collective-permute-start | bytes 454664 | tf_op jit(solution)/shard_map/ppermute | solution.py:413
  48.9 9.7 %collective-permute-start.2 = (s32[152,128]{1,0:T(8,128)}, s32[152,128]{1,0:T(8,128)S(1)}, u32[]{:S(2)}, u32[]{:S(2)}) collective-permute-start(s32[152,128]{1,0:T(8,128)} %get-tuple-element.38), channel_id=1, source_target_pairs={{0,12},{4,8},{8,4},{12,0},{16,28},{20,24},{24,20},{28,16},{1,13},{... | collective-permute-start | bytes 233480 | tf_op jit(solution)/shard_map/ppermute | solution.py:413
  58.7 20.4 %collective-permute-start.17 = (s32[296,128]{1,0:T(8,128)}, s32[296,128]{1,0:T(8,128)S(1)}, u32[]{:S(2)}, u32[]{:S(2)}) collective-permute-start(s32[296,128]{1,0:T(8,128)} %get-tuple-element.56), channel_id=1, source_target_pairs={{0,16},{4,20},{8,24},{12,28},{16,0},{20,4},{24,8},{28,12},{1,17},{... | collective-permute-start | bytes 454664 | tf_op jit(solution)/shard_map/ppermute | solution.py:413
  61.9 22.0 %collective-permute-start.18 = (s32[296,128]{1,0:T(8,128)}, s32[296,128]{1,0:T(8,128)S(1)}, u32[]{:S(2)}, u32[]{:S(2)}) collective-permute-start(s32[296,128]{1,0:T(8,128)} %get-tuple-element.57), channel_id=1, source_target_pairs={{0,20},{4,16},{8,28},{12,24},{16,4},{20,0},{24,12},{28,8},{1,21},{... | collective-permute-start | bytes 454664 | tf_op jit(solution)/shard_map/ppermute | solution.py:413
  62.8 26.2 %collective-permute-start.19 = (s32[296,128]{1,0:T(8,128)}, s32[296,128]{1,0:T(8,128)S(1)}, u32[]{:S(2)}, u32[]{:S(2)}) collective-permute-start(s32[296,128]{1,0:T(8,128)} %get-tuple-element.58), channel_id=1, source_target_pairs={{0,24},{4,28},{8,16},{12,20},{16,8},{20,12},{24,0},{28,4},{1,25},{... | collective-permute-start | bytes 454664 | tf_op jit(solution)/shard_map/ppermute | solution.py:413
  64.5 32.1 %collective-permute-start.20 = (s32[296,128]{1,0:T(8,128)}, s32[296,128]{1,0:T(8,128)S(1)}, u32[]{:S(2)}, u32[]{:S(2)}) collective-permute-start(s32[296,128]{1,0:T(8,128)} %get-tuple-element.59), channel_id=1, source_target_pairs={{0,28},{4,24},{8,20},{12,16},{16,12},{20,8},{24,4},{28,0},{1,29},{... | collective-permute-start | bytes 454664 | tf_op jit(solution)/shard_map/ppermute | solution.py:413
  79.0 27.2 %collective-permute-start.3 = (s32[152,128]{1,0:T(8,128)}, s32[152,128]{1,0:T(8,128)S(1)}, u32[]{:S(2)}, u32[]{:S(2)}) collective-permute-start(s32[152,128]{1,0:T(8,128)} %get-tuple-element.39), channel_id=1, source_target_pairs={{0,16},{4,20},{8,24},{12,28},{16,0},{20,4},{24,8},{28,12},{1,17},{... | collective-permute-start | bytes 233480 | tf_op jit(solution)/shard_map/ppermute | solution.py:413
  84.0 22.3 %collective-permute-start.4 = (s32[152,128]{1,0:T(8,128)}, s32[152,128]{1,0:T(8,128)S(1)}, u32[]{:S(2)}, u32[]{:S(2)}) collective-permute-start(s32[152,128]{1,0:T(8,128)} %get-tuple-element.40), channel_id=1, source_target_pairs={{0,20},{4,16},{8,28},{12,24},{16,4},{20,0},{24,12},{28,8},{1,21},{... | collective-permute-start | bytes 233480 | tf_op jit(solution)/shard_map/ppermute | solution.py:413
  89.0 17.3 %collective-permute-start.5 = (s32[152,128]{1,0:T(8,128)}, s32[152,128]{1,0:T(8,128)S(1)}, u32[]{:S(2)}, u32[]{:S(2)}) collective-permute-start(s32[152,128]{1,0:T(8,128)} %get-tuple-element.41), channel_id=1, source_target_pairs={{0,24},{4,28},{8,16},{12,20},{16,8},{20,12},{24,0},{28,4},{1,25},{... | collective-permute-start | bytes 233480 | tf_op jit(solution)/shard_map/ppermute | solution.py:413
  96.6 9.7 %collective-permute-start.6 = (s32[152,128]{1,0:T(8,128)}, s32[152,128]{1,0:T(8,128)S(1)}, u32[]{:S(2)}, u32[]{:S(2)}) collective-permute-start(s32[152,128]{1,0:T(8,128)} %get-tuple-element.42), channel_id=1, source_target_pairs={{0,28},{4,24},{8,20},{12,16},{16,12},{20,8},{24,4},{28,0},{1,29},{... | collective-permute-start | bytes 233480 | tf_op jit(solution)/shard_map/ppermute | solution.py:413
  98.7 1.0 copy-start.1
  99.8 1.0 copy-start.4
  100.8 0.7 copy-start.12
  101.5 0.7 copy-start.15
  102.2 0.9 copy-start.16
  103.1 3.2 %copy-start.2 = (bf16[512,512]{1,0:T(8,128)(2,1)S(1)}, bf16[512,512]{1,0:T(8,128)(2,1)}, u32[]{:S(2)}) copy-start(bf16[512,512]{1,0:T(8,128)(2,1)} %constant.15.clone.refs_9_.refs_10_) | copy-start | bytes 1572868
  106.3 0.9 copy-start.5
  107.2 0.7 copy-start.13
where the time goes:
time: 121 us; the launch traced here: 120 us
  starting transfers between devices  39.6 us (33%)
  waiting for transfers between devices  31 us (26%)
  Pallas kernels  27 us (22%)
  local copies, waits for them, and re-layouts  13.2 us (11%)
  blocking collectives  9.43 us (8%)
    ppermute x21, starting transfers between devices, swap(): return lax.ppermute(block, axis, [(i, i ^ distance) for i in devices])  38.3 us
    ppermute x21, waiting for transfers between devices, swap(): return lax.ppermute(block, axis, [(i, i ^ distance) for i in devices])  31 us
    pallas_call x3, Pallas kernels, fold(): call(functools.partial(send, z, chunk, len(inputs)), [SMEM] * (at == 0) +...  17.9 us
    unnamed x34, local copies, waits for them, and re-layouts  13.2 us
    all_to_all x1, blocking collectives, per_device(): lax.all_to_all(power, 'tm', split_axis=0, concat_axis=0, tiled=True)  9.43 us
    pallas_call x3, Pallas kernels, taken(): return call(body, specs, shapes, scratch, take_flops * count)(*values)  8.2 us
  transfers between devices with their start and end apart: 22, of which 7 were waited for; matrix products, arithmetic and copies ran while one was open for 0% of the time, Pallas kernels for 15%

commit v1 on v0

--- a/solution.py
+++ b/solution.py
@@ -17,6 +17,8 @@
 HALF = 32768.0
 VMEM_GRANT = 24 << 20
 VMEM_WHOLE = 67_043_328
+VMEM_MOST = VMEM_WHOLE - (5 << 19)
+PIECES = 3
 EXP_BIAS = 80
 BF16 = jnp.bfloat16
 F32 = jnp.float32
@@ -169,13 +171,8 @@
     return (word_real << 16) | word_imag, code_row
 
 
-def fold_and_code(z, instants, spread, slot_rank, taper_ref, real, imag, outs):
-    count = len(instants)
-    folders = [make_folder(z, instant, spread) for instant in instants]
-    folder = folders[0] if count == 1 else jnp.concatenate(folders, axis=0)
-    taper = taper_ref[...]
-    sum_real = dot(folder, real) * taper
-    sum_imag = dot(folder, imag) * taper
+def code_blocks(z, folders, slot_rank, sum_real, sum_imag, outs):
+    count = len(folders)
     rows = [] if slot_rank is None else [slot_rank]
     codes = []
     for at in range(count):
@@ -211,41 +208,46 @@
         outs[distance][count * z.data_rows :, :] = jnp.where(mine, meta, 0)
 
 
-def send(z, instants, count, *refs):
+def send(z, instants, count, copied, *refs):
     first = instants[0] == 0
     if first:
         me_ref, *refs = refs
     sources, outs, refs = refs[:count], refs[count : count + z.owners], refs[count + z.owners :]
     if first:
         spread_out, *refs = refs
-    targets, sems = refs[:count], refs[count]
-    copies = [
-        pltpu.make_async_copy(source, target, sems.at[i])
-        for i, (source, target) in enumerate(zip(sources, targets))
-    ]
-    for copy in copies:
-        copy.start()
-    for copy in copies[:-2]:
-        copy.wait()
-    *small, taper_ref, real, imag = targets
+    copies, pieces = [], [slice(0, z.rows)]
+    if copied:
+        *targets, sems = refs
+        pieces = [slice(i * z.rows // PIECES, (i + 1) * z.rows // PIECES) for i in range(PIECES)]
+        pairs = list(zip(sources[:-2], targets[:-2]))
+        for piece in pieces:
+            pairs += [(a.at[piece], b.at[piece]) for a, b in zip(sources[-2:], targets[-2:])]
+        copies = [pltpu.make_async_copy(a, b, sems.at[i]) for i, (a, b) in enumerate(pairs)]
+        for copy in copies:
+            copy.start()
+        for copy in copies[: count - 2]:
+            copy.wait()
+        sources = targets
+    *small, taper_ref, real, imag = sources
     if first:
         spread, slot_rank = place_groups(z, me_ref[0], *small)
         spread_out[...] = spread
     else:
         spread, slot_rank = small[0][...], None
-    for copy in copies[-2:]:
-        copy.wait()
-    flat = (z.fold, z.channels)
-    fold_and_code(
-        z,
-        instants,
-        spread,
-        slot_rank,
-        taper_ref,
-        real[...].reshape(flat),
-        imag[...].reshape(flat),
-        outs,
-    )
+    folders = [make_folder(z, instant, spread) for instant in instants]
+    folder = folders[0] if len(folders) == 1 else jnp.concatenate(folders, axis=0)
+    sum_real = sum_imag = None
+    for at, piece in enumerate(pieces):
+        for copy in copies[count - 2 + 2 * at : count + 2 * at]:
+            copy.wait()
+        depth = (piece.stop - piece.start) * z.times
+        left = folder[:, piece.start * z.times : piece.stop * z.times]
+        part_real = dot(left, real[piece].reshape(depth, z.channels))
+        part_imag = dot(left, imag[piece].reshape(depth, z.channels))
+        sum_real = part_real if at == 0 else sum_real + part_real
+        sum_imag = part_imag if at == 0 else sum_imag + part_imag
+    taper = taper_ref[...]
+    code_blocks(z, folders, slot_rank, sum_real * taper, sum_imag * taper, outs)
 
 
 def sum_meta(z, blocks, count):
@@ -331,7 +333,11 @@
 
 
 def take(z, kind, count, names, *refs):
-    held, (*outs, words) = dict(zip(names, refs[: len(names)])), refs[len(names) :]
+    refs = list(refs)
+    me_ref = refs.pop(0) if kind == "last" else None
+    held, refs = dict(zip(names, refs[: len(names)])), refs[len(names) :]
+    power = refs.pop() if kind == "last" else None
+    *outs, words = refs
     blocks = [held[f"block{d}"] for d in range(z.owners)]
     meta = sum_meta(z, blocks, count)
     first = kind == "first"
@@ -356,14 +362,18 @@
         outs[0][...] = spectra[-1]
         outs[1][...] = total
         return
-    outs[0][...] = total + product(z, spectra[-1], held["following"][...])
-
-
-def finish(z, parts, out):
+    power[...] = total + product(z, spectra[-1], held["following"][...])
     size = RADIX * z.share
-    total = parts[:size]
-    for part in range(1, z.parts):
-        total = total + parts[part * size : (part + 1) * size]
+    for distance in range(z.parts):
+        start = pl.multiple_of((me_ref[0] ^ distance) * size, SUBLANES)
+        outs[distance][...] = power[pl.ds(start, size), :]
+
+
+def finish(z, *refs):
+    *parts, out = refs
+    total = parts[0][...]
+    for part in parts[1:]:
+        total = total + part[...]
     width = z.short // RADIX
     rows = []
     for block in range(RADIX):
@@ -428,6 +438,7 @@
         lax.axis_size("tm"),
     )
     me = lax.axis_index("bl").astype(I32).reshape(1)
+    my_part = lax.axis_index("tm").astype(I32).reshape(1)
     taper = jnp.asarray(taper_table(channels))
     high, low = (jnp.asarray(table) for table in short_tables(z.short))
     twiddle = jnp.asarray(twiddle_table(channels))
@@ -447,14 +458,18 @@
 
     def fold(at, inputs, extra_outs):
         chunk = chunks[at]
+        copied = True
+        scratch = []
+        if copied:
+            scratch = [pltpu.VMEM(value.shape, value.dtype) for value in inputs]
+            scratch.append(pltpu.SemaphoreType.DMA((len(inputs) - 2 + 2 * PIECES,)))
         return call(
-            functools.partial(send, z, chunk, len(inputs)),
-            [SMEM] * (at == 0) + [HBM] * len(inputs),
+            functools.partial(send, z, chunk, len(inputs), copied),
+            [SMEM] * (at == 0) + [HBM if copied else VMEM] * len(inputs),
             sends(chunk) + extra_outs,
-            [pltpu.VMEM(value.shape, value.dtype) for value in inputs]
-            + [pltpu.SemaphoreType.DMA((len(inputs),))],
+            scratch,
             fold_flops * len(chunk),
-            grant=VMEM_WHOLE,
+            grant=VMEM_MOST if at else VMEM_WHOLE,
         )(*([me] * (at == 0)), *inputs)
 
     large = (taper, visibility_real, visibility_imag)
@@ -470,6 +485,7 @@
         arrived.append(exchange(fold(at, (spread,) + large, [])))
 
     spec_shape = jax.ShapeDtypeStruct((RADIX * z.per_owner, 2 * z.short), F32)
+    part_shape = jax.ShapeDtypeStruct((RADIX * z.share, z.short), F32)
     power_shape = jax.ShapeDtypeStruct((RADIX * z.per_owner, z.short), F32)
     take_flops = 3 * 2 * RADIX * z.per_owner * (2 * z.short) ** 2
     state = {"twiddle": twiddle, "high": high, "low": low}
@@ -480,6 +496,10 @@
         values = list(inputs.values())
         scratch = [pltpu.VMEM((z.slots, channels), I32)]
         specs = [VMEM] * len(values)
+        if kind == "last":
+            specs = [SMEM] + specs
+            values = [my_part] + values
+            scratch.append(pltpu.VMEM(power_shape.shape, F32))
         count = len(chunks[at])
         body = functools.partial(take, z, kind, count, names)
         return call(body, specs, shapes, scratch, take_flops * count)(*values)
@@ -493,20 +513,20 @@
             "middle", 1, [spec_shape, power_shape], state | {"ranks": ranks, "prior": spec}
         )
         running = {"running": power}
-    (power,) = taken(
+    shares = taken(
         "last",
         len(chunks) - 1,
-        [power_shape],
+        [part_shape] * z.parts,
         {"ranks": ranks} | state | {"prior": spec, "following": following} | running,
     )
-    gathered = lax.all_to_all(power, "tm", split_axis=0, concat_axis=0, tiled=True)
+    moved = [swap(shares[d], "tm", d) for d in range(1, z.parts)]
     return call(
         functools.partial(finish, z),
-        [VMEM],
+        [VMEM] * z.parts,
         jax.ShapeDtypeStruct((z.share, channels), F32),
         [],
         1 << 20,
-    )(gathered)
+    )(shares[0], *moved)
 
 
 def solution(mesh):

time: 121 us -> 104 us (0.86)
  the two profiles are of different devices: /device:TPU:10 before, /device:TPU:9 now
where the time goes in v1:
time: 104 us
  waiting for transfers between devices  38.4 us (37%)
  starting transfers between devices  37.9 us (36%)
  Pallas kernels  21.7 us (21%)
  local copies, waits for them, and re-layouts  5.66 us (5%)
    ppermute x24, waiting for transfers between devices, swap(): return lax.ppermute(block, axis, [(i, i ^ distance) for i in devices])  38.4 us
    ppermute x24, starting transfers between devices, swap(): return lax.ppermute(block, axis, [(i, i ^ distance) for i in devices])  33.3 us
    pallas_call x3, Pallas kernels, fold(): call(functools.partial(send, z, chunk, len(inputs), copied), [SMEM] * (at...  16.6 us
    unnamed x28, local copies, waits for them, and re-layouts  5.66 us
    ppermute x1, starting transfers between devices, per_device(): lax.ppermute(spec, 'tm', [(i, i - 1) for i in range(1, z.parts)])  4.53 us
    pallas_call x3, Pallas kernels, taken(): return call(body, specs, shapes, scratch, take_flops * count)(*values)  4.19 us
  transfers between devices with their start and end apart: 25, of which 9 were waited for; matrix products, arithmetic and copies ran while one was open for 0% of the time, Pallas kernels for 14%

profile of v1, /device:TPU:9, one launch (start us, length us, event | category | flops | bytes accessed | tf_op | source)
XLA Modules:
  0.0 103.8 jit_solution(17353134826633953055)
XLA Ops:
  0.0 5.1 %shard_map.91 = (s32[152,128]{1,0:T(8,128)}, s32[152,128]{1,0:T(8,128)}, s32[152,128]{1,0:T(8,128)}, s32[152,128]{1,0:T(8,128)}, s32[152,128]{1,0:T(8,128)}, /*i...) custom-call(s32[1]{0:T(128)} %bitcast.1.refs_0_, s32[3,128]{1,0:T(4,128)} %bitcast.6, ...), custom_call_target="tpu_custom_call" | custom-call | flops 905969664 | bytes 1048576 | tf_op jit(solution)/shard_map/pallas_call | solution.py:466
  5.1 2.4 %collective-permute-start.10 = (s32[152,128]{1,0:T(8,128)}, s32[152,128]{1,0:T(8,128)S(1)}, u32[]{:S(2)}, u32[]{:S(2)}) collective-permute-start(s32[152,128]{1,0:T(8,128)} %get-tuple-element.51), channel_id=1, source_target_pairs={{0,16},{4,20},{8,24},{12,28},{16,0},{20,4},{24,8},{28,12},{1,17},{... | collective-permute-start | bytes 233480 | tf_op jit(solution)/shard_map/ppermute | solution.py:423
  7.5 1.0 collective-permute-start.11
  8.5 1.3 %collective-permute-start.12 = (s32[152,128]{1,0:T(8,128)}, s32[152,128]{1,0:T(8,128)S(1)}, u32[]{:S(2)}, u32[]{:S(2)}) collective-permute-start(s32[152,128]{1,0:T(8,128)} %get-tuple-element.53), channel_id=1, source_target_pairs={{0,24},{4,28},{8,16},{12,20},{16,8},{20,12},{24,0},{28,4},{1,25},{... | collective-permute-start | bytes 233480 | tf_op jit(solution)/shard_map/ppermute | solution.py:423
  9.8 0.2 collective-permute-start.13
  9.9 1.2 %collective-permute-start.7 = (s32[152,128]{1,0:T(8,128)}, s32[152,128]{1,0:T(8,128)S(1)}, u32[]{:S(2)}, u32[]{:S(2)}) collective-permute-start(s32[152,128]{1,0:T(8,128)} %get-tuple-element.48), channel_id=1, source_target_pairs={{0,4},{4,0},{8,12},{12,8},{16,20},{20,16},{24,28},{28,24},{1,5},{5... | collective-permute-start | bytes 233480 | tf_op jit(solution)/shard_map/ppermute | solution.py:423
  11.1 5.1 %collective-permute-done.10.refs_4_ = s32[152,128]{1,0:T(8,128)S(1)} collective-permute-done((s32[152,128]{1,0:T(8,128)}, s32[152,128]{1,0:T(8,128)S(1)}, u32[]{:S(2)}, u32[]{:S(2)}) %collective-permute-start.10) | collective-permute-done | bytes 77856 | tf_op jit(solution)/shard_map/ppermute | solution.py:423
  16.2 0.0 collective-permute-start.8
  16.2 1.8 %collective-permute-done.11.refs_5_ = s32[152,128]{1,0:T(8,128)S(1)} collective-permute-done((s32[152,128]{1,0:T(8,128)}, s32[152,128]{1,0:T(8,128)S(1)}, u32[]{:S(2)}, u32[]{:S(2)}) %collective-permute-start.11) | collective-permute-done | bytes 77856 | tf_op jit(solution)/shard_map/ppermute | solution.py:423
  18.0 0.8 collective-permute-start.9
  18.8 5.0 %shard_map.92 = (s32[152,128]{1,0:T(8,128)}, s32[152,128]{1,0:T(8,128)}, s32[152,128]{1,0:T(8,128)}, s32[152,128]{1,0:T(8,128)}, s32[152,128]{1,0:T(8,128)}, /*i...) custom-call(s32[16,1536]{1,0:T(8,128)} %get-tuple-element.38.refs_0_, ...), custom_call_target="tpu_custom_call" | custom-call | flops 905969664 | bytes 1048576 | tf_op jit(solution)/shard_map/pallas_call | solution.py:466
  23.9 1.3 %collective-permute-start = (s32[152,128]{1,0:T(8,128)}, s32[152,128]{1,0:T(8,128)S(1)}, u32[]{:S(2)}, u32[]{:S(2)}) collective-permute-start(s32[152,128]{1,0:T(8,128)} %get-tuple-element.40), channel_id=1, source_target_pairs={{0,4},{4,0},{8,12},{12,8},{16,20},{20,16},{24,28},{28,24},{1,5},{5... | collective-permute-start | bytes 233480 | tf_op jit(solution)/shard_map/ppermute | solution.py:423
  25.2 0.6 collective-permute-start.1
  25.8 1.1 %shard_map.93 = (f32[256,512]{1,0:T(8,128)S(1)}, s32[8,128]{1,0:T(8,128)S(1)}) custom-call(s32[152,128]{1,0:T(8,128)S(1)} %copy-done.3, s32[152,128]{1,0:T(8,128)S(1)} %collective-permute-done.7.refs_1_, s32[152,128]{1,0:T(8,128)S(1)} %collective-permute-done.8.refs_2_, s32[152,128]{1,0:T(8,128)S(1)} %collective-permute-done.9.refs_3_, ...), custom_call_target="tpu_custom_call" | custom-call | flops 402653184 | bytes 1048576 | tf_op jit(solution)/shard_map/pallas_call | solution.py:505
  26.9 4.5 %collective-permute-start.21 = (f32[256,512]{1,0:T(8,128)S(1)}, f32[256,512]{1,0:T(8,128)S(1)}, u32[]{:S(2)}, u32[]{:S(2)}) collective-permute-start(f32[256,512]{1,0:T(8,128)S(1)} %get-tuple-element.64.refs_12_), channel_id=1, source_target_pairs={{1,0},{2,1},{3,2},{5,4},{6,5},{7,6},{9,8},{10,9},{11,10},{13,12},{... | collective-permute-start | bytes 1572872 | tf_op jit(solution)/shard_map/ppermute | solution.py:509
  31.5 6.5 %shard_map.94 = (s32[296,128]{1,0:T(8,128)}, s32[296,128]{1,0:T(8,128)}, s32[296,128]{1,0:T(8,128)}, s32[296,128]{1,0:T(8,128)}, s32[296,128]{1,0:T(8,128)}, /*i...) custom-call(s32[16,1536]{1,0:T(8,128)} %get-tuple-element.38.refs_0_, ...), custom_call_target="tpu_custom_call" | custom-call | flops 1811939328 | bytes 1048576 | tf_op jit(solution)/shard_map/pallas_call | solution.py:466
  38.0 0.6 collective-permute-start.14
  38.6 1.7 %collective-permute-start.15 = (s32[296,128]{1,0:T(8,128)}, s32[296,128]{1,0:T(8,128)S(1)}, u32[]{:S(2)}, u32[]{:S(2)}) collective-permute-start(s32[296,128]{1,0:T(8,128)} %get-tuple-element.58), channel_id=1, source_target_pairs={{0,8},{4,12},{8,0},{12,4},{16,24},{20,28},{24,16},{28,20},{1,9},{5... | collective-permute-start | bytes 454664 | tf_op jit(solution)/shard_map/ppermute | solution.py:423
  40.3 0.6 collective-permute-start.16
  41.0 1.7 %collective-permute-start.2 = (s32[152,128]{1,0:T(8,128)S(1)}, s32[152,128]{1,0:T(8,128)S(1)}, u32[]{:S(2)}, u32[]{:S(2)}) collective-permute-start(s32[152,128]{1,0:T(8,128)S(1)} %copy-done.13), channel_id=1, source_target_pairs={{0,12},{4,8},{8,4},{12,0},{16,28},{20,24},{24,20},{28,16},{1,13},{... | collective-permute-start | bytes 233480 | tf_op jit(solution)/shard_map/ppermute | solution.py:423
  42.7 7.6 %collective-permute-done.2.refs_4_ = s32[152,128]{1,0:T(8,128)S(1)} collective-permute-done((s32[152,128]{1,0:T(8,128)S(1)}, s32[152,128]{1,0:T(8,128)S(1)}, u32[]{:S(2)}, u32[]{:S(2)}) %collective-permute-start.2) | collective-permute-done | bytes 77856 | tf_op jit(solution)/shard_map/ppermute | solution.py:423
  50.3 3.0 %collective-permute-start.17 = (s32[296,128]{1,0:T(8,128)}, s32[296,128]{1,0:T(8,128)S(1)}, u32[]{:S(2)}, u32[]{:S(2)}) collective-permute-start(s32[296,128]{1,0:T(8,128)} %get-tuple-element.60), channel_id=1, source_target_pairs={{0,16},{4,20},{8,24},{12,28},{16,0},{20,4},{24,8},{28,12},{1,17},{... | collective-permute-start | bytes 454664 | tf_op jit(solution)/shard_map/ppermute | solution.py:423
  53.3 0.1 collective-permute-start.18
  53.4 1.2 %collective-permute-start.19 = (s32[296,128]{1,0:T(8,128)}, s32[296,128]{1,0:T(8,128)S(1)}, u32[]{:S(2)}, u32[]{:S(2)}) collective-permute-start(s32[296,128]{1,0:T(8,128)} %get-tuple-element.62), channel_id=1, source_target_pairs={{0,24},{4,28},{8,16},{12,20},{16,8},{20,12},{24,0},{28,4},{1,25},{... | collective-permute-start | bytes 454664 | tf_op jit(solution)/shard_map/ppermute | solution.py:423
  54.6 1.1 %collective-permute-start.20 = (s32[296,128]{1,0:T(8,128)}, s32[296,128]{1,0:T(8,128)S(1)}, u32[]{:S(2)}, u32[]{:S(2)}) collective-permute-start(s32[296,128]{1,0:T(8,128)} %get-tuple-element.63), channel_id=1, source_target_pairs={{0,28},{4,24},{8,20},{12,16},{16,12},{20,8},{24,4},{28,0},{1,29},{... | collective-permute-start | bytes 454664 | tf_op jit(solution)/shard_map/ppermute | solution.py:423
  55.7 14.2 %collective-permute-done.17.refs_4_ = s32[296,128]{1,0:T(8,128)S(1)} collective-permute-done((s32[296,128]{1,0:T(8,128)}, s32[296,128]{1,0:T(8,128)S(1)}, u32[]{:S(2)}, u32[]{:S(2)}) %collective-permute-start.17) | collective-permute-done | bytes 151584 | tf_op jit(solution)/shard_map/ppermute | solution.py:423
  69.9 3.0 %collective-permute-start.3 = (s32[152,128]{1,0:T(8,128)}, s32[152,128]{1,0:T(8,128)S(1)}, u32[]{:S(2)}, u32[]{:S(2)}) collective-permute-start(s32[152,128]{1,0:T(8,128)} %get-tuple-element.43), channel_id=1, source_target_pairs={{0,16},{4,20},{8,24},{12,28},{16,0},{20,4},{24,8},{28,12},{1,17},{... | collective-permute-start | bytes 233480 | tf_op jit(solution)/shard_map/ppermute | solution.py:423
  72.9 1.8 %collective-permute-done.18.refs_5_ = s32[296,128]{1,0:T(8,128)S(1)} collective-permute-done((s32[296,128]{1,0:T(8,128)}, s32[296,128]{1,0:T(8,128)S(1)}, u32[]{:S(2)}, u32[]{:S(2)}) %collective-permute-start.18) | collective-permute-done | bytes 151584 | tf_op jit(solution)/shard_map/ppermute | solution.py:423
  74.6 0.7 copy-done.5
  75.3 4.0 %collective-permute-start.4 = (s32[152,128]{1,0:T(8,128)}, s32[152,128]{1,0:T(8,128)S(1)}, u32[]{:S(2)}, u32[]{:S(2)}) collective-permute-start(s32[152,128]{1,0:T(8,128)} %get-tuple-element.44), channel_id=1, source_target_pairs={{0,20},{4,16},{8,28},{12,24},{16,4},{20,0},{24,12},{28,8},{1,21},{... | collective-permute-start | bytes 233480 | tf_op jit(solution)/shard_map/ppermute | solution.py:423
  79.3 0.4 collective-permute-done.19.refs_6_
  79.7 0.7 copy-done.7
  80.4 2.1 %collective-permute-start.5 = (s32[152,128]{1,0:T(8,128)}, s32[152,128]{1,0:T(8,128)S(1)}, u32[]{:S(2)}, u32[]{:S(2)}) collective-permute-start(s32[152,128]{1,0:T(8,128)} %get-tuple-element.45), channel_id=1, source_target_pairs={{0,24},{4,28},{8,16},{12,20},{16,8},{20,12},{24,0},{28,4},{1,25},{... | collective-permute-start | bytes 233480 | tf_op jit(solution)/shard_map/ppermute | solution.py:423
  82.5 4.1 %collective-permute-done.20.refs_7_ = s32[296,128]{1,0:T(8,128)S(1)} collective-permute-done((s32[296,128]{1,0:T(8,128)}, s32[296,128]{1,0:T(8,128)S(1)}, u32[]{:S(2)}, u32[]{:S(2)}) %collective-permute-start.20) | collective-permute-done | bytes 151584 | tf_op jit(solution)/shard_map/ppermute | solution.py:423
  86.5 0.7 copy-done.9
  87.2 2.7 %collective-permute-start.6 = (s32[152,128]{1,0:T(8,128)S(1)}, s32[152,128]{1,0:T(8,128)S(1)}, u32[]{:S(2)}, u32[]{:S(2)}) collective-permute-start(s32[152,128]{1,0:T(8,128)S(1)} %copy-done.12), channel_id=1, source_target_pairs={{0,28},{4,24},{8,20},{12,16},{16,12},{20,8},{24,4},{28,0},{1,29},{... | collective-permute-start | bytes 233480 | tf_op jit(solution)/shard_map/ppermute | solution.py:423
  89.9 0.9 copy-done.6
  90.9 0.9 copy-done.8
  91.8 0.9 copy-done.10
  92.7 0.9 copy-done.11
  93.6 2.0 %shard_map.95 = (f32[256,512]{1,0:T(8,128)S(1)}, f32[256,256]{1,0:T(8,128)S(1)}) custom-call(s32[296,128]{1,0:T(8,128)S(1)} %copy-done.11, s32[296,128]{1,0:T(8,128)S(1)} %collective-permute-done.14.refs_1_, s32[296,128]{1,0:T(8,128)S(1)} %collective-permute-done.15.refs_2_, s32[296,128]{1,0:T(8,128)S(1)} %collective-permute-done.16.refs_3_, ...), custom_call_target="tpu_custom_call" | custom-call | flops 805306368 | bytes 1048576 | tf_op jit(solution)/shard_map/pallas_call | solution.py:505
  95.6 1.1 %shard_map.96 = (f32[64,256]{1,0:T(8,128)S(1)}, f32[64,256]{1,0:T(8,128)S(1)}, f32[64,256]{1,0:T(8,128)S(1)}, f32[64,256]{1,0:T(8,128)S(1)}) custom-call(s32[1]{0:T(128)} %bitcast.refs_0_, s32[152,128]{1,0:T(8,128)S(1)} %copy-done.2, s32[152,128]{1,0:T(8,128)S(1)} %collective-permute-done.refs_2_, s32[152,128]{1,0:T(8,128)S(1)} %collective-permute-done.1.refs_3_, ...), custom_call_target="tpu_custom_call" | custom-call | flops 402653184 | bytes 1048576 | tf_op jit(solution)/shard_map/pallas_call | solution.py:505
  96.8 0.9 collective-permute-start.22
  97.7 1.1 %collective-permute-start.23 = (f32[64,256]{1,0:T(8,128)S(1)}, f32[64,256]{1,0:T(8,128)S(1)}, u32[]{:S(2)}, u32[]{:S(2)}) collective-permute-start(f32[64,256]{1,0:T(8,128)S(1)} %get-tuple-element.69), channel_id=1, source_target_pairs={{0,2},{1,3},{2,0},{3,1},{4,6},{5,7},{6,4},{7,5},{8,10},{9,11},{10,... | collective-permute-start | bytes 196616 | tf_op jit(solution)/shard_map/ppermute | solution.py:423
  98.8 0.6 collective-permute-start.24
  99.4 1.9 %collective-permute-done.23.refs_2_ = f32[64,256]{1,0:T(8,128)S(1)} collective-permute-done((f32[64,256]{1,0:T(8,128)S(1)}, f32[64,256]{1,0:T(8,128)S(1)}, u32[]{:S(2)}, u32[]{:S(2)}) %collective-permute-start.23) | collective-permute-done | bytes 65568 | tf_op jit(solution)/shard_map/ppermute | solution.py:423
  101.3 1.7 %collective-permute-done.24.refs_3_ = f32[64,256]{1,0:T(8,128)S(1)} collective-permute-done((f32[64,256]{1,0:T(8,128)S(1)}, f32[64,256]{1,0:T(8,128)S(1)}, u32[]{:S(2)}, u32[]{:S(2)}) %collective-permute-start.24) | collective-permute-done | bytes 65568 | tf_op jit(solution)/shard_map/ppermute | solution.py:423
  103.0 0.9 shard_map.97
  (37 shorter events, 0.1 us)
Async XLA Ops:
  5.1 11.1 %collective-permute-start.10 = (s32[152,128]{1,0:T(8,128)}, s32[152,128]{1,0:T(8,128)S(1)}, u32[]{:S(2)}, u32[]{:S(2)}) collective-permute-start(s32[152,128]{1,0:T(8,128)} %get-tuple-element.51), channel_id=1, source_target_pairs={{0,16},{4,20},{8,24},{12,28},{16,0},{20,4},{24,8},{28,12},{1,17},{... | collective-permute-start | bytes 233480 | tf_op jit(solution)/shard_map/ppermute | solution.py:423
  7.5 10.5 %collective-permute-start.11 = (s32[152,128]{1,0:T(8,128)}, s32[152,128]{1,0:T(8,128)S(1)}, u32[]{:S(2)}, u32[]{:S(2)}) collective-permute-start(s32[152,128]{1,0:T(8,128)} %get-tuple-element.52), channel_id=1, source_target_pairs={{0,20},{4,16},{8,28},{12,24},{16,4},{20,0},{24,12},{28,8},{1,21},{... | collective-permute-start | bytes 233480 | tf_op jit(solution)/shard_map/ppermute | solution.py:423
  8.5 15.4 %collective-permute-start.12 = (s32[152,128]{1,0:T(8,128)}, s32[152,128]{1,0:T(8,128)S(1)}, u32[]{:S(2)}, u32[]{:S(2)}) collective-permute-start(s32[152,128]{1,0:T(8,128)} %get-tuple-element.53), channel_id=1, source_target_pairs={{0,24},{4,28},{8,16},{12,20},{16,8},{20,12},{24,0},{28,4},{1,25},{... | collective-permute-start | bytes 233480 | tf_op jit(solution)/shard_map/ppermute | solution.py:423
  9.8 15.4 %collective-permute-start.13 = (s32[152,128]{1,0:T(8,128)}, s32[152,128]{1,0:T(8,128)S(1)}, u32[]{:S(2)}, u32[]{:S(2)}) collective-permute-start(s32[152,128]{1,0:T(8,128)} %get-tuple-element.54), channel_id=1, source_target_pairs={{0,28},{4,24},{8,20},{12,16},{16,12},{20,8},{24,4},{28,0},{1,29},{... | collective-permute-start | bytes 233480 | tf_op jit(solution)/shard_map/ppermute | solution.py:423
  9.9 15.8 %collective-permute-start.7 = (s32[152,128]{1,0:T(8,128)}, s32[152,128]{1,0:T(8,128)S(1)}, u32[]{:S(2)}, u32[]{:S(2)}) collective-permute-start(s32[152,128]{1,0:T(8,128)} %get-tuple-element.48), channel_id=1, source_target_pairs={{0,4},{4,0},{8,12},{12,8},{16,20},{20,16},{24,28},{28,24},{1,5},{5... | collective-permute-start | bytes 233480 | tf_op jit(solution)/shard_map/ppermute | solution.py:423
  16.2 9.6 %collective-permute-start.8 = (s32[152,128]{1,0:T(8,128)}, s32[152,128]{1,0:T(8,128)S(1)}, u32[]{:S(2)}, u32[]{:S(2)}) collective-permute-start(s32[152,128]{1,0:T(8,128)} %get-tuple-element.49), channel_id=1, source_target_pairs={{0,8},{4,12},{8,0},{12,4},{16,24},{20,28},{24,16},{28,20},{1,9},{5... | collective-permute-start | bytes 233480 | tf_op jit(solution)/shard_map/ppermute | solution.py:423
  18.0 7.8 %collective-permute-start.9 = (s32[152,128]{1,0:T(8,128)}, s32[152,128]{1,0:T(8,128)S(1)}, u32[]{:S(2)}, u32[]{:S(2)}) collective-permute-start(s32[152,128]{1,0:T(8,128)} %get-tuple-element.50), channel_id=1, source_target_pairs={{0,12},{4,8},{8,4},{12,0},{16,28},{20,24},{24,20},{28,16},{1,13},{... | collective-permute-start | bytes 233480 | tf_op jit(solution)/shard_map/ppermute | solution.py:423
  18.8 6.9 %copy-start = (bf16[512,512]{1,0:T(8,128)(2,1)S(1)}, bf16[512,512]{1,0:T(8,128)(2,1)}, u32[]{:S(2)}) copy-start(bf16[512,512]{1,0:T(8,128)(2,1)} %constant.18.clone.refs_9_.refs_11_) | copy-start | bytes 1572868
  18.8 7.0 %copy-start.1 = (bf16[512,512]{1,0:T(8,128)(2,1)S(1)}, bf16[512,512]{1,0:T(8,128)(2,1)}, u32[]{:S(2)}) copy-start(bf16[512,512]{1,0:T(8,128)(2,1)} %constant.19.clone.refs_10_.refs_12_) | copy-start | bytes 1572868
  18.8 7.0 %copy-start.3 = (s32[152,128]{1,0:T(8,128)S(1)}, s32[152,128]{1,0:T(8,128)}, u32[]{:S(2)}) copy-start(s32[152,128]{1,0:T(8,128)} %get-tuple-element.47.refs_0_) | copy-start | bytes 233476
  18.8 7.0 %copy-start.4 = (f32[8,256]{1,0:T(8,128)S(1)}, f32[8,256]{1,0:T(8,128)}, u32[]{:S(2)}) copy-start(f32[8,256]{1,0:T(8,128)} %constant.20.clone.refs_8_.refs_10_) | copy-start | bytes 24580
  23.9 16.5 %collective-permute-start = (s32[152,128]{1,0:T(8,128)}, s32[152,128]{1,0:T(8,128)S(1)}, u32[]{:S(2)}, u32[]{:S(2)}) collective-permute-start(s32[152,128]{1,0:T(8,128)} %get-tuple-element.40), channel_id=1, source_target_pairs={{0,4},{4,0},{8,12},{12,8},{16,20},{20,16},{24,28},{28,24},{1,5},{5... | collective-permute-start | bytes 233480 | tf_op jit(solution)/shard_map/ppermute | solution.py:423
  25.2 15.8 %collective-permute-start.1 = (s32[152,128]{1,0:T(8,128)}, s32[152,128]{1,0:T(8,128)S(1)}, u32[]{:S(2)}, u32[]{:S(2)}) collective-permute-start(s32[152,128]{1,0:T(8,128)} %get-tuple-element.41), channel_id=1, source_target_pairs={{0,8},{4,12},{8,0},{12,4},{16,24},{20,28},{24,16},{28,20},{1,9},{5... | collective-permute-start | bytes 233480 | tf_op jit(solution)/shard_map/ppermute | solution.py:423
  26.9 14.1 %copy-start.13 = (s32[152,128]{1,0:T(8,128)S(1)}, s32[152,128]{1,0:T(8,128)}, u32[]{:S(2)}) copy-start(s32[152,128]{1,0:T(8,128)} %get-tuple-element.42) | copy-start | bytes 233476
  26.9 60.3 %copy-start.12 = (s32[152,128]{1,0:T(8,128)S(1)}, s32[152,128]{1,0:T(8,128)}, u32[]{:S(2)}) copy-start(s32[152,128]{1,0:T(8,128)} %get-tuple-element.46) | copy-start | bytes 233476
  26.9 68.7 %copy-start.2 = (s32[152,128]{1,0:T(8,128)S(1)}, s32[152,128]{1,0:T(8,128)}, u32[]{:S(2)}) copy-start(s32[152,128]{1,0:T(8,128)} %get-tuple-element.39.refs_1_) | copy-start | bytes 233476
  26.9 68.7 %collective-permute-start.21 = (f32[256,512]{1,0:T(8,128)S(1)}, f32[256,512]{1,0:T(8,128)S(1)}, u32[]{:S(2)}, u32[]{:S(2)}) collective-permute-start(f32[256,512]{1,0:T(8,128)S(1)} %get-tuple-element.64.refs_12_), channel_id=1, source_target_pairs={{1,0},{2,1},{3,2},{5,4},{6,5},{7,6},{9,8},{10,9},{11,10},{13,12},{... | collective-permute-start | bytes 1572872 | tf_op jit(solution)/shard_map/ppermute | solution.py:509
  38.0 15.3 %collective-permute-start.14 = (s32[296,128]{1,0:T(8,128)}, s32[296,128]{1,0:T(8,128)S(1)}, u32[]{:S(2)}, u32[]{:S(2)}) collective-permute-start(s32[296,128]{1,0:T(8,128)} %get-tuple-element.57), channel_id=1, source_target_pairs={{0,4},{4,0},{8,12},{12,8},{16,20},{20,16},{24,28},{28,24},{1,5},{5... | collective-permute-start | bytes 454664 | tf_op jit(solution)/shard_map/ppermute | solution.py:423
  38.6 14.8 %collective-permute-start.15 = (s32[296,128]{1,0:T(8,128)}, s32[296,128]{1,0:T(8,128)S(1)}, u32[]{:S(2)}, u32[]{:S(2)}) collective-permute-start(s32[296,128]{1,0:T(8,128)} %get-tuple-element.58), channel_id=1, source_target_pairs={{0,8},{4,12},{8,0},{12,4},{16,24},{20,28},{24,16},{28,20},{1,9},{5... | collective-permute-start | bytes 454664 | tf_op jit(solution)/shard_map/ppermute | solution.py:423
  40.3 14.3 %collective-permute-start.16 = (s32[296,128]{1,0:T(8,128)}, s32[296,128]{1,0:T(8,128)S(1)}, u32[]{:S(2)}, u32[]{:S(2)}) collective-permute-start(s32[296,128]{1,0:T(8,128)} %get-tuple-element.59), channel_id=1, source_target_pairs={{0,12},{4,8},{8,4},{12,0},{16,28},{20,24},{24,20},{28,16},{1,13},{... | collective-permute-start | bytes 454664 | tf_op jit(solution)/shard_map/ppermute | solution.py:423
  41.0 9.3 %collective-permute-start.2 = (s32[152,128]{1,0:T(8,128)S(1)}, s32[152,128]{1,0:T(8,128)S(1)}, u32[]{:S(2)}, u32[]{:S(2)}) collective-permute-start(s32[152,128]{1,0:T(8,128)S(1)} %copy-done.13), channel_id=1, source_target_pairs={{0,12},{4,8},{8,4},{12,0},{16,28},{20,24},{24,20},{28,16},{1,13},{... | collective-permute-start | bytes 233480 | tf_op jit(solution)/shard_map/ppermute | solution.py:423
  50.3 19.6 %collective-permute-start.17 = (s32[296,128]{1,0:T(8,128)}, s32[296,128]{1,0:T(8,128)S(1)}, u32[]{:S(2)}, u32[]{:S(2)}) collective-permute-start(s32[296,128]{1,0:T(8,128)} %get-tuple-element.60), channel_id=1, source_target_pairs={{0,16},{4,20},{8,24},{12,28},{16,0},{20,4},{24,8},{28,12},{1,17},{... | collective-permute-start | bytes 454664 | tf_op jit(solution)/shard_map/ppermute | solution.py:423
  53.3 21.3 %collective-permute-start.18 = (s32[296,128]{1,0:T(8,128)}, s32[296,128]{1,0:T(8,128)S(1)}, u32[]{:S(2)}, u32[]{:S(2)}) collective-permute-start(s32[296,128]{1,0:T(8,128)} %get-tuple-element.61), channel_id=1, source_target_pairs={{0,20},{4,16},{8,28},{12,24},{16,4},{20,0},{24,12},{28,8},{1,21},{... | collective-permute-start | bytes 454664 | tf_op jit(solution)/shard_map/ppermute | solution.py:423
  53.4 26.3 %collective-permute-start.19 = (s32[296,128]{1,0:T(8,128)}, s32[296,128]{1,0:T(8,128)S(1)}, u32[]{:S(2)}, u32[]{:S(2)}) collective-permute-start(s32[296,128]{1,0:T(8,128)} %get-tuple-element.62), channel_id=1, source_target_pairs={{0,24},{4,28},{8,16},{12,20},{16,8},{20,12},{24,0},{28,4},{1,25},{... | collective-permute-start | bytes 454664 | tf_op jit(solution)/shard_map/ppermute | solution.py:423
  54.6 31.9 %collective-permute-start.20 = (s32[296,128]{1,0:T(8,128)}, s32[296,128]{1,0:T(8,128)S(1)}, u32[]{:S(2)}, u32[]{:S(2)}) collective-permute-start(s32[296,128]{1,0:T(8,128)} %get-tuple-element.63), channel_id=1, source_target_pairs={{0,28},{4,24},{8,20},{12,16},{16,12},{20,8},{24,4},{28,0},{1,29},{... | collective-permute-start | bytes 454664 | tf_op jit(solution)/shard_map/ppermute | solution.py:423
  69.9 25.7 %collective-permute-start.3 = (s32[152,128]{1,0:T(8,128)}, s32[152,128]{1,0:T(8,128)S(1)}, u32[]{:S(2)}, u32[]{:S(2)}) collective-permute-start(s32[152,128]{1,0:T(8,128)} %get-tuple-element.43), channel_id=1, source_target_pairs={{0,16},{4,20},{8,24},{12,28},{16,0},{20,4},{24,8},{28,12},{1,17},{... | collective-permute-start | bytes 233480 | tf_op jit(solution)/shard_map/ppermute | solution.py:423
  74.6 0.7 copy-start.5
  75.3 20.3 %collective-permute-start.4 = (s32[152,128]{1,0:T(8,128)}, s32[152,128]{1,0:T(8,128)S(1)}, u32[]{:S(2)}, u32[]{:S(2)}) collective-permute-start(s32[152,128]{1,0:T(8,128)} %get-tuple-element.44), channel_id=1, source_target_pairs={{0,20},{4,16},{8,28},{12,24},{16,4},{20,0},{24,12},{28,8},{1,21},{... | collective-permute-start | bytes 233480 | tf_op jit(solution)/shard_map/ppermute | solution.py:423
  79.7 0.7 copy-start.7
  80.4 15.2 %collective-permute-start.5 = (s32[152,128]{1,0:T(8,128)}, s32[152,128]{1,0:T(8,128)S(1)}, u32[]{:S(2)}, u32[]{:S(2)}) collective-permute-start(s32[152,128]{1,0:T(8,128)} %get-tuple-element.45), channel_id=1, source_target_pairs={{0,24},{4,28},{8,16},{12,20},{16,8},{20,12},{24,0},{28,4},{1,25},{... | collective-permute-start | bytes 233480 | tf_op jit(solution)/shard_map/ppermute | solution.py:423
  86.5 0.7 copy-start.9
  87.2 8.4 %collective-permute-start.6 = (s32[152,128]{1,0:T(8,128)S(1)}, s32[152,128]{1,0:T(8,128)S(1)}, u32[]{:S(2)}, u32[]{:S(2)}) collective-permute-start(s32[152,128]{1,0:T(8,128)S(1)} %copy-done.12), channel_id=1, source_target_pairs={{0,28},{4,24},{8,20},{12,16},{16,12},{20,8},{24,4},{28,0},{1,29},{... | collective-permute-start | bytes 233480 | tf_op jit(solution)/shard_map/ppermute | solution.py:423
  89.9 0.9 copy-start.6
  90.9 0.9 copy-start.8
  91.8 0.9 copy-start.10
  92.7 0.9 copy-start.11
  96.8 2.6 %collective-permute-start.22 = (f32[64,256]{1,0:T(8,128)S(1)}, f32[64,256]{1,0:T(8,128)S(1)}, u32[]{:S(2)}, u32[]{:S(2)}) collective-permute-start(f32[64,256]{1,0:T(8,128)S(1)} %get-tuple-element.68), channel_id=1, source_target_pairs={{0,1},{1,0},{2,3},{3,2},{4,5},{5,4},{6,7},{7,6},{8,9},{9,8},{10,11... | collective-permute-start | bytes 196616 | tf_op jit(solution)/shard_map/ppermute | solution.py:423
  97.7 3.6 %collective-permute-start.23 = (f32[64,256]{1,0:T(8,128)S(1)}, f32[64,256]{1,0:T(8,128)S(1)}, u32[]{:S(2)}, u32[]{:S(2)}) collective-permute-start(f32[64,256]{1,0:T(8,128)S(1)} %get-tuple-element.69), channel_id=1, source_target_pairs={{0,2},{1,3},{2,0},{3,1},{4,6},{5,7},{6,4},{7,5},{8,10},{9,11},{10,... | collective-permute-start | bytes 196616 | tf_op jit(solution)/shard_map/ppermute | solution.py:423
  98.8 4.2 %collective-permute-start.24 = (f32[64,256]{1,0:T(8,128)S(1)}, f32[64,256]{1,0:T(8,128)S(1)}, u32[]{:S(2)}, u32[]{:S(2)}) collective-permute-start(f32[64,256]{1,0:T(8,128)S(1)} %get-tuple-element.70), channel_id=1, source_target_pairs={{0,3},{1,2},{2,1},{3,0},{4,7},{5,6},{6,5},{7,4},{8,11},{9,10},{10,... | collective-permute-start | bytes 196616 | tf_op jit(solution)/shard_map/ppermute | solution.py:423
